TPU v7x, 32 devices: a whole 2x2x4 slice. The times are simulated.
32 devices in a mesh: lat: 16 (over z, x, core), lev: 2 (over y).
Axes of the slice: x: 2, y: 2, z: 4, core: 2. Of those that a mesh axis runs over, the one named last changes fastest.
Arguments:
- anomalies: bfloat16 [4, 2, 80, 32, 1536], P(None, 'lev', None, 'lat'), may hold values from -6 to 6
- error_now: float32 [4, 2, 32, 1536], P(None, 'lev', 'lat'), may hold values from -6 to 6
- error_prior: float32 [4, 2, 32, 1536], P(None, 'lev', 'lat'), may hold values from -4.2 to 4.2
- energy_coef: float32 [4, 2], P(None, 'lev'), may hold values from 0.3 to 3
- obs_anomalies: bfloat16 [2048, 80, 256], P('lat', 'lev'), may hold values from -6 to 6
- innovations: float32 [2048, 256], P('lat'), may hold values from -6 to 6
- valid_counts: int32 [2048], P('lat'), may hold values from 0 to 256, as said below
- type_ids: int32 [2048], P('lat'), may hold values from 0 to 7
- error_inverse: float32 [8], replicated, may hold values from 0.25 to 4
Outputs:
- impact: float32 [2048, 16, 256], P('lat', 'lev')
- type_totals: float32 [16, 8], P('lev')
Inputs may be any that keep to these rules, and one draw needn't show every extreme that they name: `valid_counts`: among the 128 slots of each index of lat, the blocks with a positive count come first and the first is always positive; in every draw some index of lat has all 128 slots positive and some block holds 256 rows. Rows below a block's count are observations, the rest padding.
All inputs are finite; a program needn't handle non-finite values.
Results may differ from a plain program's by a relative error of at most 0.0042.
Values may be sent and summed in bfloat16 or wider, within the bound.
No kernel may reach another device: no remote copies, remote signals or barrier semaphores. Data moves between devices by JAX's collectives and lax.ppermute only.
A program may use at most 64 MiB of HBM per device.

v0:
```python
import math
import jax
import jax.numpy as jnp
from jax import lax
from jax.sharding import PartitionSpec as P

NLAT_GRID = 768
LAT0 = 256
REGIONS = 4
NTYPES = 8


def local(
    anomalies,
    error_now,
    error_prior,
    energy_coef,
    obs_anomalies,
    innovations,
    valid_counts,
    type_ids,
    error_inverse,
):
    lat_rows = error_now.shape[2]
    lat_total = lat_rows * lax.axis_size("lat")
    lev_total = error_now.shape[1] * lax.axis_size("lev")
    lon_count = error_now.shape[3]
    lat_index = lax.axis_index("lat") * lat_rows + jnp.arange(lat_rows, dtype=jnp.int32)
    cosine = jnp.cos(
        -0.5 * math.pi + ((lat_index + LAT0).astype(jnp.float32) + 0.5) * math.pi / NLAT_GRID
    )
    gradient = (
        energy_coef[:, :, None, None] * cosine[None, None, :, None] * (error_now + error_prior)
    ).astype(jnp.bfloat16)
    folded = jnp.einsum("vlkji,vlji->vkj", anomalies, gradient, preferred_element_type=jnp.float32)
    region = lat_index * REGIONS // lat_total
    onehot = (region[None, :] == jnp.arange(REGIONS, dtype=jnp.int32)[:, None]).astype(jnp.float32)
    partial_value = jnp.einsum("vkj,rj->vkr", folded, onehot, precision=lax.Precision.HIGHEST)
    summed = lax.psum(partial_value, ("lat", "lev"))
    members = anomalies.shape[2]
    norm_scale = math.sqrt(lev_total * lat_total * lon_count / REGIONS)
    weights = (jnp.transpose(summed, (1, 0, 2)).reshape(members, -1) / norm_scale).astype(
        jnp.bfloat16
    )
    slot_count, local_members, block_rows = obs_anomalies.shape
    lev_groups = lax.axis_size("lev")
    grouped = obs_anomalies.reshape(lev_groups, slot_count // lev_groups, local_members, block_rows)
    answered = jnp.einsum(
        "gbks,kt->gbts",
        lax.all_to_all(grouped, "lev", split_axis=0, concat_axis=2, tiled=True),
        weights,
        preferred_element_type=jnp.float32,
    )
    response = lax.all_to_all(answered[0], "lev", split_axis=1, concat_axis=0, tiled=True)
    type_table = type_ids[:, None] == jnp.arange(NTYPES, dtype=jnp.int32)[None, :]
    inverse_var = jnp.sum(
        jnp.where(type_table, error_inverse[None, :], jnp.zeros((), jnp.float32)), axis=1
    )
    positions = jnp.arange(block_rows, dtype=jnp.int32)
    row_mask = (positions[None, :] < valid_counts[:, None]).astype(jnp.float32)
    scaling = innovations * inverse_var[:, None] * row_mask / math.sqrt(members - 1)
    impact = response * scaling[:, None, :]
    per_block = jnp.sum(impact, axis=2)
    local_totals = jnp.dot(
        per_block.T, type_table.astype(jnp.float32), precision=lax.Precision.HIGHEST
    )
    block_total = slot_count * lax.axis_size("lat")
    type_totals = lax.psum(local_totals, "lat") / math.sqrt(block_total * block_rows / NTYPES)
    return (impact, type_totals)


def solution(mesh):
    in_specs = (
        P(None, "lev", None, "lat", None),
        P(None, "lev", "lat", None),
        P(None, "lev", "lat", None),
        P(None, "lev"),
        P("lat", "lev", None),
        P("lat", None),
        P("lat"),
        P("lat"),
        P(),
    )
    out_specs = (P("lat", "lev", None), P("lev", None))
    return jax.shard_map(local, mesh=mesh, in_specs=in_specs, out_specs=out_specs, check_vma=False)
```

profile of v0, /device:TPU:0, one launch (start us, length us, event | category | flops | bytes accessed | tf_op | source)
XLA Modules:
  0.0 126.0 jit_solution(2320645867197905039)
XLA Ops:
  0.6 0.0 copy-start
  0.6 0.0 copy-start.6
  0.7 0.0 copy-start.2
  0.7 0.0 copy-start.3
  0.7 5.2 %all-to-all-start = ((bf16[2,64,40,256]{3,2,1,0:T(8,128)(2,1)}), bf16[2,64,40,256]{3,2,1,0:T(8,128)(2,1)}, u32[]{:S(2)}, u32[]{:S(2)}) async-start(bf16[2,64,40,256]{3,2,1,0:T(8,128)(2,1)} %bitcast.48), calls=%async_computation | async-start | bytes 5242880 | tf_op jit(solution)/shard_map/all_to_all | solution.py:50
  5.9 0.0 copy-done.6
  5.9 0.1 broadcast_multiply_fusion.1
  6.0 0.0 copy-done.2
  6.0 0.0 copy-done.3
  6.0 0.1 fusion.4
  6.1 0.6 fusion
  6.7 0.3 fusion.7
  7.0 65.6 %psum.14 = f32[4,80,4]{1,2,0:T(4,128)S(1)} all-reduce(f32[4,80,4]{1,2,0:T(4,128)S(1)} %fusion.7), channel_id=1, replica_groups=mesh['lat'=16,'lev'=2] {'lat','lev'}, use_global_device_ids=true, to_apply=%region_0.1 | all-reduce | flops 1280 | bytes 10240 | tf_op jit(solution)/shard_map/psum | solution.py:39
  72.5 0.0 all-to-all-done
  72.5 1.9 %copy.25 = bf16[1,64,2,40,256]{4,3,2,1,0:T(8,128)(2,1)S(1)} copy(bf16[1,64,2,40,256]{4,3,1,2,0:T(8,128)(2,1)} %bitcast.13) | data formatting | bytes 5242880 | tf_op jit(solution)/shard_map/all_to_all | solution.py:50
  74.5 0.5 convolution_bitcast_fusion
  74.9 0.0 copy-start.1
  75.0 0.0 copy-start.4
  75.0 1.6 %copy.26 = f32[64,16,256]{2,0,1:T(8,128)} copy(f32[64,16,256]{2,1,0:T(8,128)S(1)} %convolution_bitcast_fusion) | data formatting | bytes 2097152 | tf_op jit(solution)/shard_map/squeeze | solution.py:54
  76.6 3.6 %all-to-all-start.1 = ((f32[64,16,256]{2,0,1:T(8,128)}), f32[64,16,256]{2,0,1:T(8,128)S(1)}, u32[]{:S(2)}, u32[]{:S(2)}) async-start(f32[64,16,256]{2,0,1:T(8,128)} %copy.26), calls=%async_computation.1 | async-start | bytes 2097152 | tf_op jit(solution)/shard_map/all_to_all | solution.py:54
  80.2 0.1 select_reduce_fusion
  80.3 0.1 select_multiply_fusion
  80.4 0.1 copy.29
  80.5 12.7 %all-to-all-done.1 = f32[64,16,256]{2,0,1:T(8,128)S(1)} async-done(((f32[64,16,256]{2,0,1:T(8,128)}), f32[64,16,256]{2,0,1:T(8,128)S(1)}, u32[]{:S(2)}, u32[]{:S(2)}) %all-to-all-start.1) | async-done | bytes 1048608 | tf_op jit(solution)/shard_map/all_to_all | solution.py:54
  93.2 0.7 fusion.2
  93.9 0.1 copy.30
  94.0 0.1 reduce_sum.22
  94.1 0.1 fusion.5
  94.2 29.5 %psum.15 = f32[8,8]{1,0:T(8,128)S(1)} all-reduce(f32[8,8]{1,0:T(8,128)S(1)} %fusion.5), channel_id=1, replica_groups=mesh['lat'=16,'lev'=2] {'lat'}, use_global_device_ids=true, to_apply=%region_3.4 | all-reduce | flops 64 | bytes 512 | tf_op jit(solution)/shard_map/psum | solution.py:68
  123.7 0.6 broadcast_multiply_fusion
  124.3 0.6 copy.28
  124.9 1.1 bitcast_multiply_fusion
  (10 shorter events, 0.1 us)
Async XLA Ops:
  0.6 5.5 %copy-start = (bf16[4,1,80,2,1536]{4,3,2,1,0:T(2,128)(2,1)S(1)}, bf16[4,1,80,2,1536]{4,3,2,1,0:T(2,128)(2,1)}, u32[]{:S(2)}) copy-start(bf16[4,1,80,2,1536]{4,3,2,1,0:T(2,128)(2,1)} %param.9) | copy-start | bytes 5898244
  0.6 5.3 %copy-start.6 = (f32[4,1]{0,1:T(1,128)S(1)}, f32[4,1]{0,1:T(1,128)}, u32[]{:S(2)}) copy-start(f32[4,1]{0,1:T(1,128)} %param.12) | copy-start | bytes 52
  0.7 5.3 %copy-start.2 = (f32[4,1,2,1536]{3,2,1,0:T(2,128)S(1)}, f32[4,1,2,1536]{3,2,1,0:T(2,128)}, u32[]{:S(2)}) copy-start(f32[4,1,2,1536]{3,2,1,0:T(2,128)} %param.10) | copy-start | bytes 147460
  0.7 5.3 %copy-start.3 = (f32[4,1,2,1536]{3,2,1,0:T(2,128)S(1)}, f32[4,1,2,1536]{3,2,1,0:T(2,128)}, u32[]{:S(2)}) copy-start(f32[4,1,2,1536]{3,2,1,0:T(2,128)} %param.11) | copy-start | bytes 147460
  0.7 71.9 %all-to-all-start = ((bf16[2,64,40,256]{3,2,1,0:T(8,128)(2,1)}), bf16[2,64,40,256]{3,2,1,0:T(8,128)(2,1)}, u32[]{:S(2)}, u32[]{:S(2)}) async-start(bf16[2,64,40,256]{3,2,1,0:T(8,128)(2,1)} %bitcast.48), calls=%async_computation | async-start | bytes 5242880 | tf_op jit(solution)/shard_map/all_to_all | solution.py:50
  74.9 5.2 %copy-start.5 = (s32[128]{0:T(128)S(1)}, s32[128]{0:T(128)}, u32[]{:S(2)}) copy-start(s32[128]{0:T(128)} %param.16) | copy-start | bytes 1540
  74.9 5.2 %copy-start.7 = (f32[8]{0:T(128)S(1)}, f32[8]{0:T(128)}, u32[]{:S(2)}) copy-start(f32[8]{0:T(128)} %param.17) | copy-start | bytes 100
  74.9 5.3 %copy-start.1 = (f32[128,256]{1,0:T(8,128)S(1)}, f32[128,256]{1,0:T(8,128)}, u32[]{:S(2)}) copy-start(f32[128,256]{1,0:T(8,128)} %param.14) | copy-start | bytes 393220
  75.0 5.3 %copy-start.4 = (s32[128]{0:T(128)S(1)}, s32[128]{0:T(128)}, u32[]{:S(2)}) copy-start(s32[128]{0:T(128)} %param.15) | copy-start | bytes 1540
  76.6 16.6 %all-to-all-start.1 = ((f32[64,16,256]{2,0,1:T(8,128)}), f32[64,16,256]{2,0,1:T(8,128)S(1)}, u32[]{:S(2)}, u32[]{:S(2)}) async-start(f32[64,16,256]{2,0,1:T(8,128)} %copy.26), calls=%async_computation.1 | async-start | bytes 2097152 | tf_op jit(solution)/shard_map/all_to_all | solution.py:54
where the time goes:
time: 126 us
  blocking collectives  95 us (75%)
  waiting for transfers between devices  12.7 us (10%)
  starting transfers between devices  8.74 us (7%)
  local copies, waits for them, and re-layouts  4.43 us (4%)
  other arithmetic  2.83 us (2%)
  matrix products  1.44 us (1%)
    psum x1, blocking collectives, local(): summed = lax.psum(partial_value, ('lat', 'lev'))  65.6 us
    psum x1, blocking collectives, local(): lax.psum(local_totals, 'lat') / math.sqrt(block_total * block_rows / NTYPES)  29.5 us
    all_to_all x1, waiting for transfers between devices, local(): lax.all_to_all(answered[0], 'lev', split_axis=1, concat_axis=0, tiled=True)  12.7 us
    all_to_all x1, starting transfers between devices, local(): lax.all_to_all(grouped, 'lev', split_axis=0, concat_axis=2, tiled=True)  5.16 us
    all_to_all x1, starting transfers between devices, local(): lax.all_to_all(answered[0], 'lev', split_axis=1, concat_axis=0, tiled=True)  3.58 us
  transfers between devices with their start and end apart: 2, of which 1 were waited for; matrix products, arithmetic and copies ran while one was open for 1% of the time, Pallas kernels for 0%

commit v1 on v0

--- a/solution.py
+++ b/solution.py
@@ -36,7 +36,7 @@
     region = lat_index * REGIONS // lat_total
     onehot = (region[None, :] == jnp.arange(REGIONS, dtype=jnp.int32)[:, None]).astype(jnp.float32)
     partial_value = jnp.einsum("vkj,rj->vkr", folded, onehot, precision=lax.Precision.HIGHEST)
-    summed = lax.psum(partial_value, ("lat", "lev"))
+    summed = lax.psum(lax.psum(partial_value, "lev"), "lat")
     members = anomalies.shape[2]
     norm_scale = math.sqrt(lev_total * lat_total * lon_count / REGIONS)
     weights = (jnp.transpose(summed, (1, 0, 2)).reshape(members, -1) / norm_scale).astype(

time: 126 us -> 124 us (0.984)
  waiting for transfers between devices: 12.7 us -> 10.5 us
    all_to_all x1, waiting for transfers between devices: 12.7 us -> 10.5 us  [local(): lax.all_to_all(answered[0], 'lev', split_axis=1, concat_axis=0, tiled=True)]
    psum x1 -> x2, blocking collectives: 65.6 us -> 64.4 us  [local(): summed = lax.psum(lax.psum(partial_value, 'lev'), 'lat')]
where the time goes in v1:
time: 124 us; the launch traced here: 123 us
  blocking collectives  94.5 us (76%)
  waiting for transfers between devices  10.5 us (8%)
  starting transfers between devices  8.73 us (7%)
  local copies, waits for them, and re-layouts  4.43 us (4%)
  other arithmetic  2.83 us (2%)
  matrix products  1.44 us (1%)
    psum x2, blocking collectives, local(): summed = lax.psum(lax.psum(partial_value, 'lev'), 'lat')  64.4 us
    psum x1, blocking collectives, local(): lax.psum(local_totals, 'lat') / math.sqrt(block_total * block_rows / NTYPES)  30.1 us
    all_to_all x1, waiting for transfers between devices, local(): lax.all_to_all(answered[0], 'lev', split_axis=1, concat_axis=0, tiled=True)  10.5 us
    all_to_all x1, starting transfers between devices, local(): lax.all_to_all(grouped, 'lev', split_axis=0, concat_axis=2, tiled=True)  5.15 us
    all_to_all x1, starting transfers between devices, local(): lax.all_to_all(answered[0], 'lev', split_axis=1, concat_axis=0, tiled=True)  3.58 us
  transfers between devices with their start and end apart: 2, of which 1 were waited for; matrix products, arithmetic and copies ran while one was open for 1% of the time, Pallas kernels for 0%

profile of v1, /device:TPU:0, one launch (start us, length us, event | category | flops | bytes accessed | tf_op | source)
XLA Modules:
  0.0 123.3 jit_solution(17289023685601091887)
XLA Ops:
  0.6 0.0 copy-start
  0.6 0.0 copy-start.6
  0.7 5.1 %all-to-all-start = ((bf16[2,64,40,256]{3,2,1,0:T(8,128)(2,1)}), bf16[2,64,40,256]{3,2,1,0:T(8,128)(2,1)}, u32[]{:S(2)}, u32[]{:S(2)}) async-start(bf16[2,64,40,256]{3,2,1,0:T(8,128)(2,1)} %bitcast.48), calls=%async_computation | async-start | bytes 5242880 | tf_op jit(solution)/shard_map/all_to_all | solution.py:50
  5.9 0.0 copy-done.6
  5.9 0.1 broadcast_multiply_fusion.1
  6.0 0.0 copy-done.2
  6.0 0.0 copy-done.3
  6.0 0.1 fusion.4
  6.1 0.6 fusion
  6.7 0.3 fusion.7
  7.0 31.1 %psum.21 = f32[4,80,4]{1,2,0:T(4,128)S(1)} all-reduce(f32[4,80,4]{1,2,0:T(4,128)S(1)} %fusion.7), channel_id=1, replica_groups=mesh['lat'=16,'lev'=2] {'lev'}, use_global_device_ids=true, to_apply=%region_0.1 | all-reduce | flops 1280 | bytes 10240 | tf_op jit(solution)/shard_map/psum | solution.py:39
  38.0 33.4 %psum.22 = f32[4,80,4]{1,2,0:T(4,128)S(1)} all-reduce(f32[4,80,4]{1,2,0:T(4,128)S(1)} %psum.21), channel_id=1, replica_groups=mesh['lat'=16,'lev'=2] {'lat'}, use_global_device_ids=true, to_apply=%region_1.2 | all-reduce | flops 1280 | bytes 10240 | tf_op jit(solution)/shard_map/psum | solution.py:39
  71.4 0.0 all-to-all-done
  71.4 1.9 %copy.25 = bf16[1,64,2,40,256]{4,3,2,1,0:T(8,128)(2,1)S(1)} copy(bf16[1,64,2,40,256]{4,3,1,2,0:T(8,128)(2,1)} %bitcast.13) | data formatting | bytes 5242880 | tf_op jit(solution)/shard_map/all_to_all | solution.py:50
  73.4 0.5 convolution_bitcast_fusion
  73.8 0.0 copy-start.1
  73.8 0.0 copy-start.4
  73.9 1.6 %copy.26 = f32[64,16,256]{2,0,1:T(8,128)} copy(f32[64,16,256]{2,1,0:T(8,128)S(1)} %convolution_bitcast_fusion) | data formatting | bytes 2097152 | tf_op jit(solution)/shard_map/squeeze | solution.py:54
  75.4 3.6 %all-to-all-start.1 = ((f32[64,16,256]{2,0,1:T(8,128)}), f32[64,16,256]{2,0,1:T(8,128)S(1)}, u32[]{:S(2)}, u32[]{:S(2)}) async-start(f32[64,16,256]{2,0,1:T(8,128)} %copy.26), calls=%async_computation.1 | async-start | bytes 2097152 | tf_op jit(solution)/shard_map/all_to_all | solution.py:54
  79.0 0.1 select_reduce_fusion
  79.1 0.0 copy-done.4
  79.1 0.1 select_multiply_fusion
  79.2 0.1 copy.29
  79.4 10.5 %all-to-all-done.1 = f32[64,16,256]{2,0,1:T(8,128)S(1)} async-done(((f32[64,16,256]{2,0,1:T(8,128)}), f32[64,16,256]{2,0,1:T(8,128)S(1)}, u32[]{:S(2)}, u32[]{:S(2)}) %all-to-all-start.1) | async-done | bytes 1048608 | tf_op jit(solution)/shard_map/all_to_all | solution.py:54
  89.9 0.7 fusion.2
  90.6 0.1 copy.30
  90.7 0.1 reduce_sum.22
  90.8 0.1 fusion.5
  90.9 30.1 %psum.23 = f32[8,8]{1,0:T(8,128)S(1)} all-reduce(f32[8,8]{1,0:T(8,128)S(1)} %fusion.5), channel_id=1, replica_groups=mesh['lat'=16,'lev'=2] {'lat'}, use_global_device_ids=true, to_apply=%region_4.5 | all-reduce | flops 64 | bytes 512 | tf_op jit(solution)/shard_map/psum | solution.py:68
  121.0 0.6 broadcast_multiply_fusion
  121.6 0.6 copy.28
  122.2 1.1 bitcast_multiply_fusion
  (11 shorter events, 0.1 us)
Async XLA Ops:
  0.6 5.5 %copy-start = (bf16[4,1,80,2,1536]{4,3,2,1,0:T(2,128)(2,1)S(1)}, bf16[4,1,80,2,1536]{4,3,2,1,0:T(2,128)(2,1)}, u32[]{:S(2)}) copy-start(bf16[4,1,80,2,1536]{4,3,2,1,0:T(2,128)(2,1)} %param.9) | copy-start | bytes 5898244
  0.6 5.2 %copy-start.6 = (f32[4,1]{0,1:T(1,128)S(1)}, f32[4,1]{0,1:T(1,128)}, u32[]{:S(2)}) copy-start(f32[4,1]{0,1:T(1,128)} %param.12) | copy-start | bytes 52
  0.7 5.3 %copy-start.2 = (f32[4,1,2,1536]{3,2,1,0:T(2,128)S(1)}, f32[4,1,2,1536]{3,2,1,0:T(2,128)}, u32[]{:S(2)}) copy-start(f32[4,1,2,1536]{3,2,1,0:T(2,128)} %param.10) | copy-start | bytes 147460
  0.7 5.3 %copy-start.3 = (f32[4,1,2,1536]{3,2,1,0:T(2,128)S(1)}, f32[4,1,2,1536]{3,2,1,0:T(2,128)}, u32[]{:S(2)}) copy-start(f32[4,1,2,1536]{3,2,1,0:T(2,128)} %param.11) | copy-start | bytes 147460
  0.7 70.7 %all-to-all-start = ((bf16[2,64,40,256]{3,2,1,0:T(8,128)(2,1)}), bf16[2,64,40,256]{3,2,1,0:T(8,128)(2,1)}, u32[]{:S(2)}, u32[]{:S(2)}) async-start(bf16[2,64,40,256]{3,2,1,0:T(8,128)(2,1)} %bitcast.48), calls=%async_computation | async-start | bytes 5242880 | tf_op jit(solution)/shard_map/all_to_all | solution.py:50
  73.8 5.2 %copy-start.5 = (s32[128]{0:T(128)S(1)}, s32[128]{0:T(128)}, u32[]{:S(2)}) copy-start(s32[128]{0:T(128)} %param.16) | copy-start | bytes 1540
  73.8 5.2 %copy-start.7 = (f32[8]{0:T(128)S(1)}, f32[8]{0:T(128)}, u32[]{:S(2)}) copy-start(f32[8]{0:T(128)} %param.17) | copy-start | bytes 100
  73.8 5.3 %copy-start.1 = (f32[128,256]{1,0:T(8,128)S(1)}, f32[128,256]{1,0:T(8,128)}, u32[]{:S(2)}) copy-start(f32[128,256]{1,0:T(8,128)} %param.14) | copy-start | bytes 393220
  73.8 5.3 %copy-start.4 = (s32[128]{0:T(128)S(1)}, s32[128]{0:T(128)}, u32[]{:S(2)}) copy-start(s32[128]{0:T(128)} %param.15) | copy-start | bytes 1540
  75.4 14.5 %all-to-all-start.1 = ((f32[64,16,256]{2,0,1:T(8,128)}), f32[64,16,256]{2,0,1:T(8,128)S(1)}, u32[]{:S(2)}, u32[]{:S(2)}) async-start(f32[64,16,256]{2,0,1:T(8,128)} %copy.26), calls=%async_computation.1 | async-start | bytes 2097152 | tf_op jit(solution)/shard_map/all_to_all | solution.py:54

commit v2 on v0

--- a/solution.py
+++ b/solution.py
@@ -36,7 +36,7 @@
     region = lat_index * REGIONS // lat_total
     onehot = (region[None, :] == jnp.arange(REGIONS, dtype=jnp.int32)[:, None]).astype(jnp.float32)
     partial_value = jnp.einsum("vkj,rj->vkr", folded, onehot, precision=lax.Precision.HIGHEST)
-    summed = lax.psum(partial_value, ("lat", "lev"))
+    summed = jnp.sum(lax.all_gather(partial_value, ("lat", "lev")), axis=0)
     members = anomalies.shape[2]
     norm_scale = math.sqrt(lev_total * lat_total * lon_count / REGIONS)
     weights = (jnp.transpose(summed, (1, 0, 2)).reshape(members, -1) / norm_scale).astype(

time: 126 us -> 151 us (1.20)
  blocking collectives: 95 us -> 121 us
  waiting for transfers between devices: 12.7 us -> 10.8 us
    all_gather x0 -> x1, blocking collectives: none -> 91.9 us  [local(): summed = jnp.sum(lax.all_gather(partial_value, ('lat', 'lev')), axis=0)]
    psum x1 -> x0, blocking collectives: 65.6 us -> none  [local(): summed = lax.psum(partial_value, ('lat', 'lev'))]
    all_to_all x1, waiting for transfers between devices: 12.7 us -> 10.8 us  [local(): lax.all_to_all(answered[0], 'lev', split_axis=1, concat_axis=0, tiled=True)]
where the time goes in v2:
time: 151 us; the launch traced here: 150 us
  blocking collectives  121 us (80%)
  waiting for transfers between devices  10.8 us (7%)
  starting transfers between devices  8.74 us (6%)
  local copies, waits for them, and re-layouts  4.43 us (3%)
  other arithmetic  2.91 us (2%)
    all_gather x1, blocking collectives, local(): summed = jnp.sum(lax.all_gather(partial_value, ('lat', 'lev')), axis=0)  91.9 us
    psum x1, blocking collectives, local(): lax.psum(local_totals, 'lat') / math.sqrt(block_total * block_rows / NTYPES)  29.5 us
    all_to_all x1, waiting for transfers between devices, local(): lax.all_to_all(answered[0], 'lev', split_axis=1, concat_axis=0, tiled=True)  10.8 us
    all_to_all x1, starting transfers between devices, local(): lax.all_to_all(grouped, 'lev', split_axis=0, concat_axis=2, tiled=True)  5.16 us
    all_to_all x1, starting transfers between devices, local(): lax.all_to_all(answered[0], 'lev', split_axis=1, concat_axis=0, tiled=True)  3.58 us
  transfers between devices with their start and end apart: 2, of which 1 were waited for; matrix products, arithmetic and copies ran while one was open for 1% of the time, Pallas kernels for 0%

profile of v2, /device:TPU:0, one launch (start us, length us, event | category | flops | bytes accessed | tf_op | source)
XLA Modules:
  0.0 150.5 jit_solution(16024920354035923288)
XLA Ops:
  0.6 0.0 copy-start
  0.6 0.0 copy-start.6
  0.7 0.0 copy-start.2
  0.7 0.0 copy-start.3
  0.7 5.2 %all-to-all-start = ((bf16[2,64,40,256]{3,2,1,0:T(8,128)(2,1)}), bf16[2,64,40,256]{3,2,1,0:T(8,128)(2,1)}, u32[]{:S(2)}, u32[]{:S(2)}) async-start(bf16[2,64,40,256]{3,2,1,0:T(8,128)(2,1)} %bitcast.49), calls=%async_computation | async-start | bytes 5242880 | tf_op jit(solution)/shard_map/all_to_all | solution.py:50
  5.9 0.0 copy-done.6
  5.9 0.1 broadcast_multiply_fusion.1
  6.0 0.1 fusion.4
  6.1 0.6 fusion
  6.7 0.3 fusion.7
  7.0 91.9 %all-gather = f32[128,80,4]{1,2,0:T(4,128)S(1)} all-gather(f32[4,80,4]{1,2,0:T(4,128)S(1)} %fusion.7), channel_id=2, replica_groups=mesh['lat'=16,'lev'=2] {'lat','lev'}, dimensions={0}, use_global_device_ids=true | all-gather | bytes 168960 | tf_op jit(solution)/shard_map/all_gather | solution.py:39
  98.9 0.1 reduce_sum.29
  99.0 0.0 all-to-all-done
  99.0 1.9 %copy.25 = bf16[1,64,2,40,256]{4,3,2,1,0:T(8,128)(2,1)S(1)} copy(bf16[1,64,2,40,256]{4,3,1,2,0:T(8,128)(2,1)} %bitcast.14) | data formatting | bytes 5242880 | tf_op jit(solution)/shard_map/all_to_all | solution.py:50
  100.9 0.5 convolution_bitcast_fusion
  101.4 0.0 copy-start.1
  101.4 0.0 copy-start.4
  101.4 1.6 %copy.26 = f32[64,16,256]{2,0,1:T(8,128)} copy(f32[64,16,256]{2,1,0:T(8,128)S(1)} %convolution_bitcast_fusion) | data formatting | bytes 2097152 | tf_op jit(solution)/shard_map/squeeze | solution.py:54
  103.0 3.6 %all-to-all-start.1 = ((f32[64,16,256]{2,0,1:T(8,128)}), f32[64,16,256]{2,0,1:T(8,128)S(1)}, u32[]{:S(2)}, u32[]{:S(2)}) async-start(f32[64,16,256]{2,0,1:T(8,128)} %copy.26), calls=%async_computation.1 | async-start | bytes 2097152 | tf_op jit(solution)/shard_map/all_to_all | solution.py:54
  106.6 0.1 select_reduce_fusion
  106.7 0.0 copy-done.1
  106.7 0.1 select_multiply_fusion
  106.8 0.1 copy.29
  106.9 10.8 %all-to-all-done.1 = f32[64,16,256]{2,0,1:T(8,128)S(1)} async-done(((f32[64,16,256]{2,0,1:T(8,128)}), f32[64,16,256]{2,0,1:T(8,128)S(1)}, u32[]{:S(2)}, u32[]{:S(2)}) %all-to-all-start.1) | async-done | bytes 1048608 | tf_op jit(solution)/shard_map/all_to_all | solution.py:54
  117.7 0.7 fusion.2
  118.4 0.1 copy.30
  118.5 0.1 reduce_sum.32
  118.6 0.1 fusion.5
  118.7 29.5 %psum.7 = f32[8,8]{1,0:T(8,128)S(1)} all-reduce(f32[8,8]{1,0:T(8,128)S(1)} %fusion.5), channel_id=1, replica_groups=mesh['lat'=16,'lev'=2] {'lat'}, use_global_device_ids=true, to_apply=%region_3.4 | all-reduce | flops 64 | bytes 512 | tf_op jit(solution)/shard_map/psum | solution.py:68
  148.2 0.6 broadcast_multiply_fusion
  148.8 0.6 copy.28
  149.4 1.1 bitcast_multiply_fusion
  (11 shorter events, 0.1 us)
Async XLA Ops:
  0.6 5.5 %copy-start = (bf16[4,1,80,2,1536]{4,3,2,1,0:T(2,128)(2,1)S(1)}, bf16[4,1,80,2,1536]{4,3,2,1,0:T(2,128)(2,1)}, u32[]{:S(2)}) copy-start(bf16[4,1,80,2,1536]{4,3,2,1,0:T(2,128)(2,1)} %param.9) | copy-start | bytes 5898244
  0.6 5.3 %copy-start.6 = (f32[4,1]{0,1:T(1,128)S(1)}, f32[4,1]{0,1:T(1,128)}, u32[]{:S(2)}) copy-start(f32[4,1]{0,1:T(1,128)} %param.12) | copy-start | bytes 52
  0.7 5.3 %copy-start.2 = (f32[4,1,2,1536]{3,2,1,0:T(2,128)S(1)}, f32[4,1,2,1536]{3,2,1,0:T(2,128)}, u32[]{:S(2)}) copy-start(f32[4,1,2,1536]{3,2,1,0:T(2,128)} %param.10) | copy-start | bytes 147460
  0.7 5.3 %copy-start.3 = (f32[4,1,2,1536]{3,2,1,0:T(2,128)S(1)}, f32[4,1,2,1536]{3,2,1,0:T(2,128)}, u32[]{:S(2)}) copy-start(f32[4,1,2,1536]{3,2,1,0:T(2,128)} %param.11) | copy-start | bytes 147460
  0.7 98.3 %all-to-all-start = ((bf16[2,64,40,256]{3,2,1,0:T(8,128)(2,1)}), bf16[2,64,40,256]{3,2,1,0:T(8,128)(2,1)}, u32[]{:S(2)}, u32[]{:S(2)}) async-start(bf16[2,64,40,256]{3,2,1,0:T(8,128)(2,1)} %bitcast.49), calls=%async_computation | async-start | bytes 5242880 | tf_op jit(solution)/shard_map/all_to_all | solution.py:50
  101.4 5.2 %copy-start.5 = (s32[128]{0:T(128)S(1)}, s32[128]{0:T(128)}, u32[]{:S(2)}) copy-start(s32[128]{0:T(128)} %param.16) | copy-start | bytes 1540
  101.4 5.2 %copy-start.7 = (f32[8]{0:T(128)S(1)}, f32[8]{0:T(128)}, u32[]{:S(2)}) copy-start(f32[8]{0:T(128)} %param.17) | copy-start | bytes 100
  101.4 5.3 %copy-start.1 = (f32[128,256]{1,0:T(8,128)S(1)}, f32[128,256]{1,0:T(8,128)}, u32[]{:S(2)}) copy-start(f32[128,256]{1,0:T(8,128)} %param.14) | copy-start | bytes 393220
  101.4 5.3 %copy-start.4 = (s32[128]{0:T(128)S(1)}, s32[128]{0:T(128)}, u32[]{:S(2)}) copy-start(s32[128]{0:T(128)} %param.15) | copy-start | bytes 1540
  103.0 14.7 %all-to-all-start.1 = ((f32[64,16,256]{2,0,1:T(8,128)}), f32[64,16,256]{2,0,1:T(8,128)S(1)}, u32[]{:S(2)}, u32[]{:S(2)}) async-start(f32[64,16,256]{2,0,1:T(8,128)} %copy.26), calls=%async_computation.1 | async-start | bytes 2097152 | tf_op jit(solution)/shard_map/all_to_all | solution.py:54
